TPU v7x, 32 devices: a whole 2x2x4 slice. The times are simulated.
32 devices in a mesh: dp: 8 (over y, x, core), tp: 4 (over z).
Axes of the slice: x: 2, y: 2, z: 4, core: 2. Of those that a mesh axis runs over, the one named last changes fastest.
Arguments:
- inputs: bfloat16 [8, 768, 1280], P('dp', 'tp'), may hold values from -6 to 6
- saved_hidden: bfloat16 [8, 768, 5120], P('dp', None, 'tp'), may hold values from -8 to 8
- upstream: bfloat16 [8, 768, 1280], P('dp', 'tp'), may hold values from -6 to 6
- w_in: bfloat16 [1280, 5120], P(None, 'tp'), may hold values from -0.15625 to 0.15625
- w_out: bfloat16 [5120, 1280], P('tp'), may hold values from -0.078125 to 0.078125
- kernel: float32 [7, 1280], replicated, may hold values from -2 to 2
Outputs:
- grad_inputs: bfloat16 [8, 768, 1280], P('dp', 'tp')
- grad_w_in: float32 [1280, 5120], P(None, 'tp')
- grad_w_out: float32 [5120, 1280], P('tp')
- grad_bias: float32 [5120], P('tp')
- grad_kernel: float32 [7, 1280], replicated
All inputs are finite; a program needn't handle non-finite values.
Results may differ from a plain program's by a relative error of at most 0.02.
Values may be sent and summed in bfloat16 or wider, within the bound.
A program may use at most 128 MiB of HBM per device.

v0:
```python
import functools

import jax
import jax.numpy as jnp
from jax import lax
from jax.experimental import pallas as pl
from jax.experimental.pallas import tpu as pltpu
from jax.sharding import PartitionSpec as P

KW = 7
EDGE = 16
F32 = jnp.float32
BF16 = jnp.bfloat16
MESH = pl.DeviceIdType.MESH


def dot(a, b, dims):
    return lax.dot_general(a, b, (dims, ((), ())), preferred_element_type=F32)


def chunk_of(size):
    return 256 if size % 256 == 0 else size


def body(
    n, dp_size, rows_in, rows_out, up_parts, mix_parts,
    x_hbm, h_hbm, up_hbm, win_hbm, wout_hbm, k_ref, gin_ref, gk_ref, gb_ref, *refs,
):
    parts = up_parts + mix_parts
    finals, refs = refs[:parts], refs[parts:]
    accs, refs = refs[:parts], refs[parts:]
    psends, refs = refs[:parts], refs[parts:]
    precvs, refs = refs[:parts], refs[parts:]
    rsends, refs = refs[:parts], refs[parts:]
    rrecvs, refs = refs[:parts], refs[parts:]
    (
        h_ref, win_ref, wout_ref,
        act, gh, up_all, mix_all, part, zrecv, xpad, gpad, bias, k1, k2,
        ls, hl, ul, hs, hr, us, ur, zs, zr, ps, pr, rs, rr, ds, dr, gs, gr, k1s, k1r, k2s, k2r,
    ) = refs
    chips = dp_size // 2
    me = lax.axis_index("tp")
    dp = lax.axis_index("dp")
    core = lax.rem(dp, 2)
    chip = dp // 2
    tokens, width = x_hbm.shape
    hidden = h_ref.shape[2]
    up_wide = width // up_parts
    mix_wide = width // mix_parts
    tall = chunk_of(hidden)

    bits = chips.bit_length() - 1

    def mirror(i):
        return sum((i // 2**p) % 2 * 2 ** (bits - 1 - p) for p in range(bits))

    spots = (chip, mirror(chip))
    halves = [chips >> (s + 1) for s in range(bits)]
    starts = [sum(halves[:s]) for s in range(bits)]

    def span(d, s, other):
        h = halves[s]
        side = lax.rem(spots[d] // h, 2)
        low = spots[d] // h * h
        return low + (h - 2 * h * side if other else 0)

    def peer(d, s):
        h = halves[s]
        spot = spots[d] + h - 2 * h * lax.rem(spots[d] // h, 2)
        return (mirror(spot) if d else spot) * 2 + core

    partner = dp + 1 - 2 * core

    barrier = pltpu.get_barrier_semaphore()
    for j in range(1, n):
        pl.semaphore_signal(
            barrier, inc=1, device_id=(dp, lax.rem(me + j, n)), device_id_type=MESH
        )
    for j in range(1, dp_size):
        pl.semaphore_signal(
            barrier, inc=1, device_id=(lax.rem(dp + j, dp_size), me), device_id_type=MESH
        )
    pl.semaphore_wait(barrier, n - 1 + dp_size - 1)

    def send(src, dst, s, r, to):
        return pltpu.make_async_remote_copy(
            src_ref=src, dst_ref=dst, send_sem=s, recv_sem=r, device_id=to, device_id_type=MESH
        )

    pending = []

    def start(cond, make):
        if cond is None:
            make().start()
        else:

            @pl.when(cond)
            def _():
                make().start()

        pending.append((cond, make))

    ways = (0, 1)
    step_of = (1, -1)
    room = (me, n - 1 - me)
    ahead = (n - 1 - me, me)

    loads = [
        pltpu.make_async_copy(x_hbm, xpad.at[pl.ds(EDGE, tokens)], ls.at[0]),
        pltpu.make_async_copy(wout_hbm, wout_ref, ls.at[1]),
        pltpu.make_async_copy(win_hbm, win_ref, ls.at[2]),
    ]

    def load_hidden(j):
        b = lax.rem(me + j, n)
        return pltpu.make_async_copy(h_hbm.at[b], h_ref.at[b], hl.at[b])

    def load_up(c):
        src = up_hbm.at[:, pl.ds(c * up_wide, up_wide)]
        return pltpu.make_async_copy(src, up_all.at[c, me], ul.at[c])

    def place(k, b):
        return up_all.at[k, b] if k < up_parts else mix_all.at[k - up_parts, b]

    def chain(k, d, back):
        b = jnp.clip(me - step_of[d] * back, 0, n - 1)
        to = (dp, jnp.clip(me + step_of[d], 0, n - 1))
        src = place(k, b)
        if back == 0 and k < up_parts:
            src = up_hbm.at[:, pl.ds(k * up_wide, up_wide)]
        return send(src, place(k, b), us.at[k, d, b], ur.at[k, d, b], to)

    def x_edge(d):
        to = (dp, jnp.clip(me + step_of[d], 0, n - 1))
        src = x_hbm.at[pl.ds(tokens - EDGE if d == 0 else 0, EDGE)]
        dst = xpad.at[pl.ds(0 if d == 0 else EDGE + tokens, EDGE)]
        return send(src, dst, hs.at[d], hr.at[d], to)

    for d in ways:
        start(ahead[d] > 0, functools.partial(chain, 0, d, 0))
    for d in ways:
        start(ahead[d] > 0, functools.partial(x_edge, d))
    load_hidden(0).start()
    for c in range(up_parts):
        load_up(c).start()
    for load in loads:
        load.start()
    for j in range(1, n):
        load_hidden(j).start()

    if act.shape[2] > hidden:
        act[...] = jnp.zeros_like(act)
    bias[...] = jnp.zeros_like(bias)

    @pl.when(me == 0)
    def _():
        xpad[pl.ds(0, EDGE), :] = jnp.zeros((EDGE, width), BF16)
        gpad[pl.ds(0, EDGE), :] = jnp.zeros((EDGE, width), BF16)

    @pl.when(me == n - 1)
    def _():
        xpad[pl.ds(EDGE + tokens, EDGE), :] = jnp.zeros((EDGE, width), BF16)
        gpad[pl.ds(EDGE + tokens, EDGE), :] = jnp.zeros((EDGE, width), BF16)

    def gelu(b):
        pltpu.make_async_copy(h_hbm.at[b], h_ref.at[b], hl.at[b]).wait()

        def gelu_step(i, _):
            at = pl.ds(pl.multiple_of(i * 32, 32), 32)
            v = h_ref[b, at, :].astype(F32)
            cdf = 0.5 + 0.5 * lax.erf(v * 0.7071067811865476)
            act[b, at, pl.ds(0, hidden)] = (v * cdf).astype(BF16)
            gh[b, at, :] = (cdf + v * (0.3989422804014327 * jnp.exp(-0.5 * v * v))).astype(BF16)
            return 0

        lax.fori_loop(0, tokens // 32, gelu_step, 0)

    def mix():
        def mix_step(i, _):
            at = pl.ds(pl.multiple_of(i * 128, 128), 128)
            x = xpad[:, at].astype(F32)
            taps = k_ref[:, at]
            total = x[EDGE : EDGE + tokens]
            for tap in range(KW):
                low = EDGE - 3 + tap
                total = total + taps[tap : tap + 1] * x[low : low + tokens]
            c = i // (mix_wide // 128)
            lane = pl.ds(pl.multiple_of(lax.rem(i, mix_wide // 128) * 128, 128), 128)
            mix_all[c, me, :, lane] = total.astype(BF16)
            return 0

        lax.fori_loop(0, width // 128, mix_step, 0)

    def add_to(acc, at, value, first):
        if first:
            acc[at] = value
        else:
            acc[at] += value

    def out_dot(c, b, first):
        high = chunk_of(act.shape[2])

        def out_step(i, _):
            at = pl.ds(pl.multiple_of(i * high, high), high)
            value = dot(act[b, :, at], up_all[c, b], ((0,), (0,)))
            add_to(accs[c], (at, slice(None)), value, first)
            return 0

        lax.fori_loop(0, act.shape[2] // high, out_step, 0)

    def back_dot(b):
        def back_step(i, _):
            at = pl.ds(pl.multiple_of(i * tall, tall), tall) if tall < hidden else pl.ds(0, hidden)
            back = None
            for c in range(up_parts):
                cols = pl.ds(c * up_wide, up_wide)
                term = dot(up_all[c, b], wout_ref[at, cols], ((1,), (1,)))
                back = term if back is None else back + term
            grad = (gh[b, :, at].astype(F32) * back).astype(BF16)
            gh[b, :, at] = grad
            bias[:, at] += jnp.sum(grad.astype(F32), axis=0, keepdims=True)
            return 0

        lax.fori_loop(0, hidden // tall, back_step, 0)

        wide = chunk_of(width)

        def part_step(i, _):
            at = pl.ds(pl.multiple_of(i * wide, wide), wide)
            part[b, :, at] = dot(gh[b], win_ref[at, :], ((1,), (1,))).astype(BF16)
            return 0

        lax.fori_loop(0, width // wide, part_step, 0)

    def in_dot(c, b, first):
        def in_step(i, _):
            at = pl.ds(pl.multiple_of(i * 128, 128), 128)
            value = dot(mix_all[c, b, :, at], gh[b], ((0,), (0,)))
            add_to(accs[up_parts + c], (at, slice(None)), value, first)
            return 0

        lax.fori_loop(0, mix_wide // 128, in_step, 0)

    def use(k, b, first=False):
        if k < up_parts:
            if k == 0:
                gelu(b)
            out_dot(k, b, first)
            if k == up_parts - 1:
                back_dot(b)
        else:
            in_dot(k - up_parts, b, first)

    sets = [
        (accs[w], psends[w], precvs[w], rsends[w], rrecvs[w], finals[w], rows_out if w < up_parts else rows_in)
        for w in range(parts)
    ]

    def rows_at(w, half, d, block):
        rows = sets[w][6]
        return pl.ds(pl.multiple_of(((half * 2 + d) * chips + block) * rows, 8), rows)

    def pair_copy(w):
        return send(sets[w][1], sets[w][2], ps.at[w], pr.at[w], (partner, me))

    def pair_start(w):
        for d in ways:
            for block in range(chips):
                sets[w][1][d, block] = sets[w][0][rows_at(w, 1 - core, d, block), :].astype(BF16)
        start(None, functools.partial(pair_copy, w))

    def own(w, d, block):
        return sets[w][0][rows_at(w, core, d, block), :] + sets[w][2][d, block].astype(F32)

    def ring_reduce(w, d, s):
        at = pl.ds(starts[s], halves[s])
        return send(
            sets[w][3].at[d, at], sets[w][4].at[d, at], rs.at[w, d, s], rr.at[w, d, s],
            (peer(d, s), me),
        )

    def ring_gather(w, d, s, other):
        ref = sets[w][5].at[core, d, pl.ds(span(d, s, other), halves[s])]
        at = 2 * bits - 1 - s
        return send(ref, ref, rs.at[w, d, at], rr.at[w, d, at], (peer(d, s), me))

    def across(w, d, s, half):
        if s == bits:
            ref = sets[w][5].at[half, d, pl.ds(spots[d], 1)]
        else:
            ref = sets[w][5].at[half, d, pl.ds(span(d, s, True), halves[s])]
        return send(ref, ref, ds.at[w, d, s], dr.at[w, d, s], (partner, me))

    last = 2 * bits

    def ring_step(w, s):
        acc, _, _, rsend, rrecv, final, _ = sets[w]
        if s == 0:
            pair_copy(w).wait_recv()
        for d in ways:
            if s <= bits:
                if s > 0:
                    ring_reduce(w, d, s - 1).wait_recv()

                def value(block, s=s, d=d):
                    if s == 0:
                        return own(w, d, block)
                    got = rrecv[d, starts[s - 1] + block - span(d, s - 1, False)].astype(F32)
                    if s == 1:
                        return own(w, d, block) + got
                    return acc[rows_at(w, core, d, block), :] + got

                if s == bits:
                    final[core, d, spots[d]] = value(spots[d]).astype(BF16)
                    start(None, functools.partial(ring_gather, w, d, s - 1, False))
                    start(None, functools.partial(across, w, d, bits, core))
                    continue
                for j in range(halves[s]):
                    rsend[d, starts[s] + j] = value(span(d, s, True) + j).astype(BF16)
                start(None, functools.partial(ring_reduce, w, d, s))
                if s > 0:
                    for j in range(halves[s]):
                        block = span(d, s, False) + j
                        acc[rows_at(w, core, d, block), :] = value(block)
            else:
                step = 2 * bits - s
                ring_gather(w, d, step, True).wait_recv()
                if step > 0:
                    start(None, functools.partial(ring_gather, w, d, step - 1, False))
                start(None, functools.partial(across, w, d, step, core))

    def ring_end(w):
        for d in ways:
            for s in range(bits + 1):
                across(w, d, s, 1 - core).wait_recv()

    def target(d, t, behind):
        place = room[d] - behind
        block = n - 1 - t + place
        return block if d == 0 else n - 1 - block

    def z_slot(d, block, owner):
        return jnp.where((block == owner) & (d == 1), n, block)

    def z_send(d, t):
        block = jnp.clip(target(d, t, 0), 0, n - 1)
        to = jnp.clip(me + step_of[d], 0, n - 1)
        return send(
            part.at[block], zrecv.at[z_slot(d, block, to)], zs.at[d, t], zr.at[d, t], (dp, to)
        )

    def z_arrive(d, t):
        block = jnp.clip(target(d, t, 1), 0, n - 1)
        slot = zrecv.at[z_slot(d, block, me)]
        return send(slot, slot, zs.at[d, t], zr.at[d, t], (dp, jnp.clip(me + 1, 0, n - 1)))

    def z_step(t):
        if t > n - 1:
            return
        for d in ways:
            if t > 0:

                @pl.when((room[d] >= 1) & (room[d] - 1 <= t - 1))
                def _(d=d):
                    z_arrive(d, t - 1).wait_recv()
                    if t < n - 1:
                        block = jnp.clip(target(d, t - 1, 1), 0, n - 1)
                        part[block] = (
                            part[block].astype(F32) + zrecv[z_slot(d, block, me)].astype(F32)
                        ).astype(BF16)

            if t < n - 1:
                start((room[d] <= t) & (ahead[d] > 0), functools.partial(z_send, d, t))

    active = []

    def tick():
        for item in list(active):
            ring_step(item[0], item[1])
            item[1] += 1
            if item[1] > last:
                active.remove(item)

    for k in range(parts):
        follow = k + 1
        if k == 0:
            load_up(0).wait()
        use_own = functools.partial(use, k, me, True)
        if k == up_parts - 1:
            if k > 0:
                load_up(k).wait()
            loads[1].wait()
            loads[2].wait()
        use_own()
        if k == 0:
            loads[0].wait()
            for d in ways:

                @pl.when(room[d] > 0)
                def _(d=d):
                    x_edge(d).wait_recv()

            mix()
        if follow < parts:
            for d in ways:
                start((ahead[d] > 0) & (room[d] == 0), functools.partial(chain, follow, d, 0))
        for back in range(1, n):
            for d in ways:

                @pl.when(room[d] >= back)
                def _(d=d):
                    chain(k, d, back).wait_recv()

                start((room[d] >= back) & (ahead[d] > 0), functools.partial(chain, k, d, back))
                if follow < parts:
                    start((room[d] == back) & (ahead[d] > 0), functools.partial(chain, follow, d, 0))
            for d in ways:

                @pl.when(room[d] >= back)
                def _(d=d):
                    use(k, jnp.clip(me - step_of[d] * back, 0, n - 1))

            tick()
        pair_start(k)
        active.append([k, 0])
        if k >= up_parts - 1:
            z_step(k - up_parts + 1)
    for t in range(mix_parts + 1, n - 1):
        z_step(t)
        tick()
    tick()
    tick()
    tick()
    z_step(n - 1)

    def own_up(i):
        c = i // (up_wide // 128)
        lane = pl.ds(pl.multiple_of(lax.rem(i, up_wide // 128) * 128, 128), 128)
        return up_all[c, me, :, lane].astype(F32)

    def sum_step(i, _):
        at = pl.ds(pl.multiple_of(i * 128, 128), 128)
        total = part[me, :, at].astype(F32)
        left = jnp.where(me > 0, zrecv[me, :, at].astype(F32), 0.0)
        right = jnp.where(me < n - 1, zrecv[n, :, at].astype(F32), 0.0)
        gpad[pl.ds(EDGE, tokens), at] = (
            own_up(i) + (total + left + right)
        ).astype(BF16)
        return 0

    lax.fori_loop(0, width // 128, sum_step, 0)

    def g_edge(d):
        to = (dp, jnp.clip(me + step_of[d], 0, n - 1))
        src = gpad.at[pl.ds(tokens if d == 0 else EDGE, EDGE)]
        dst = gpad.at[pl.ds(0 if d == 0 else EDGE + tokens, EDGE)]
        return send(src, dst, gs.at[d], gr.at[d], to)

    for d in ways:
        start(ahead[d] > 0, functools.partial(g_edge, d))
    tick()

    def taps_step(i, _):
        at = pl.ds(pl.multiple_of(i * 128, 128), 128)
        g = gpad[pl.ds(EDGE, tokens), at].astype(F32)
        x = xpad[:, at].astype(F32)
        sums = [
            jnp.sum(g * x[EDGE - 3 + tap : EDGE - 3 + tap + tokens], axis=0, keepdims=True)
            for tap in range(KW)
        ]
        sums.append(jnp.zeros_like(sums[0]))
        k1[me, :, at] = jnp.concatenate(sums, axis=0)
        return 0

    lax.fori_loop(0, width // 128, taps_step, 0)

    def k1_send(j):
        to = lax.rem(me + j, n)
        return send(k1.at[me], k1.at[me], k1s.at[j], k1r.at[me], (dp, to))

    def k1_arrive(j):
        src = lax.rem(me + j, n)
        return send(k1.at[src], k1.at[src], k1s.at[j], k1r.at[src], (dp, src))

    for j in range(1, n):
        start(None, functools.partial(k1_send, j))
    for d in ways:

        @pl.when(room[d] > 0)
        def _(d=d):
            g_edge(d).wait_recv()

    def gin_step(i, _):
        at = pl.ds(pl.multiple_of(i * 128, 128), 128)
        g = gpad[:, at].astype(F32)
        taps = k_ref[:, at]
        total = g[EDGE : EDGE + tokens]
        for tap in range(KW):
            low = EDGE + 3 - tap
            total = total + taps[tap : tap + 1] * g[low : low + tokens]
        gin_ref[:, at] = total.astype(BF16)
        return 0

    lax.fori_loop(0, width // 128, gin_step, 0)
    tick()
    for j in range(1, n):
        k1_arrive(j).wait_recv()
    taps_sum = k1[0]
    for j in range(1, n):
        taps_sum = taps_sum + k1[j]
    k2[dp, pl.ds(0, 8), :] = taps_sum
    k2[dp, pl.ds(8, 8), pl.ds(0, hidden)] = jnp.broadcast_to(bias[...], (8, hidden))
    if hidden < width:
        k2[dp, pl.ds(8, 8), pl.ds(hidden, width - hidden)] = jnp.zeros((8, width - hidden), F32)

    def k2_send(j):
        to = lax.rem(dp + j, dp_size)
        return send(k2.at[dp], k2.at[dp], k2s.at[j], k2r.at[dp], (to, me))

    def k2_arrive(j):
        src = lax.rem(dp + j, dp_size)
        return send(k2.at[src], k2.at[src], k2s.at[j], k2r.at[src], (src, me))

    for j in range(1, dp_size):
        start(None, functools.partial(k2_send, j))
    while active:
        tick()
    for j in range(1, dp_size):
        k2_arrive(j).wait_recv()
    total = k2[0]
    for j in range(1, dp_size):
        total = total + k2[j]
    gk_ref[...] = total[:KW]
    gb_ref[...] = total[8:9, :hidden]
    for w in range(parts):
        ring_end(w)
    for cond, make in pending:
        if cond is None:
            make().wait_send()
        else:

            @pl.when(cond)
            def _(make=make):
                make().wait_send()


def shards(n, dp_size, inputs, saved_hidden, upstream, w_in, w_out, kernel):
    chips = dp_size // 2
    tokens, width = inputs.shape[1:]
    hidden = w_in.shape[1]
    up_parts = 2
    mix_parts = 2 if width % (8 * chips * 8) == 0 and width % 256 == 0 else 1
    parts = up_parts + mix_parts
    rows_in = width // (4 * chips * mix_parts)
    rows_out = -(-hidden // (4 * chips * 8)) * 8
    high = rows_out * 4 * chips
    dma = pltpu.SemaphoreType.DMA
    bits = chips.bit_length() - 1
    vmem = pl.BlockSpec(memory_space=pltpu.VMEM)
    hbm = pl.BlockSpec(memory_space=pl.ANY)
    shape = jax.ShapeDtypeStruct
    sizes = [(rows_out, width // up_parts)] * up_parts + [(rows_in, hidden)] * mix_parts
    grad_inputs, grad_kernel, grad_bias, *finals = pl.pallas_call(
        functools.partial(body, n, dp_size, rows_in, rows_out, up_parts, mix_parts),
        out_shape=[shape((tokens, width), BF16), shape((KW, width), F32), shape((1, hidden), F32)]
        + [shape((2, 2, chips) + size, BF16) for size in sizes],
        in_specs=[hbm] * 5 + [vmem],
        out_specs=[vmem] * (3 + parts),
        scratch_shapes=[pltpu.VMEM((4 * chips * r, c), F32) for r, c in sizes]
        + [pltpu.VMEM((2, chips) + size, BF16) for size in sizes] * 2
        + [pltpu.VMEM((2, chips - 1) + size, BF16) for size in sizes] * 2
        + [
            pltpu.VMEM((n, tokens, hidden), BF16),
            pltpu.VMEM((width, hidden), BF16),
            pltpu.VMEM((hidden, width), BF16),
            pltpu.VMEM((n, tokens, high), BF16),
            pltpu.VMEM((n, tokens, hidden), BF16),
            pltpu.VMEM((up_parts, n, tokens, width // up_parts), BF16),
            pltpu.VMEM((mix_parts, n, tokens, width // mix_parts), BF16),
            pltpu.VMEM((n, tokens, width), BF16),
            pltpu.VMEM((n + 1, tokens, width), BF16),
            pltpu.VMEM((tokens + 2 * EDGE, width), BF16),
            pltpu.VMEM((tokens + 2 * EDGE, width), BF16),
            pltpu.VMEM((1, hidden), F32),
            pltpu.VMEM((n, 8, width), F32),
            pltpu.VMEM((dp_size, 16, width), F32),
            dma((3,)), dma((n,)), dma((up_parts,)),
            dma((2,)), dma((2,)),
            dma((parts, 2, n)), dma((parts, 2, n)),
            dma((2, n)), dma((2, n)),
            dma((parts,)), dma((parts,)),
            dma((parts, 2, 2 * bits)), dma((parts, 2, 2 * bits)),
            dma((parts, 2, bits + 1)), dma((parts, 2, bits + 1)),
            dma((2,)), dma((2,)),
            dma((n,)), dma((n,)),
            dma((dp_size,)), dma((dp_size,)),
        ],
        compiler_params=pltpu.CompilerParams(
            collective_id=0, has_side_effects=True, vmem_limit_bytes=67043328
        ),
    )(
        inputs[0],
        saved_hidden[0].reshape(n, tokens, hidden),
        upstream[0],
        w_in,
        w_out,
        kernel,
    )
    columns = [f.reshape(high, width // up_parts)[:hidden] for f in finals[:up_parts]]
    rows = [f.reshape(width // mix_parts, hidden) for f in finals[up_parts:]]
    return (
        grad_inputs[None],
        jnp.concatenate(rows, axis=0).astype(F32),
        jnp.concatenate(columns, axis=1).astype(F32),
        grad_bias[0],
        grad_kernel,
    )


def solution(mesh):
    in_specs = (
        P("dp", "tp", None),
        P("dp", None, "tp"),
        P("dp", "tp", None),
        P(None, "tp"),
        P("tp", None),
        P(),
    )
    out_specs = (P("dp", "tp", None), P(None, "tp"), P("tp", None), P("tp"), P())
    return jax.shard_map(
        functools.partial(shards, mesh.shape["tp"], mesh.shape["dp"]),
        mesh=mesh,
        in_specs=in_specs,
        out_specs=out_specs,
        check_vma=False,
    )
```

profile of v0, /device:TPU:1, one launch (start us, length us, event | category | flops | bytes accessed | tf_op | source)
XLA Modules:
  0.0 141.4 jit_solution(15027744512539155392)
XLA Ops:
  0.6 129.8 %shard_map.101 = (bf16[192,1280]{1,0:T(8,128)(2,1)}, f32[7,1280]{1,0:T(8,128)}, f32[1,1280]{1,0:T(1,128)}, bf16[2,2,4,80,640]{4,3,2,1,0:T(8,128)(2,1)}, bf16[2,2...) custom-call(bf16[192,1280]{1,0:T(8,128)(2,1)} %bitcast.14, ...), custom_call_target="tpu_custom_call" | custom-call | tf_op jit(solution)/shard_map/pallas_call | solution.py:563
  130.4 0.0 copy-start.2
  130.4 0.0 copy-start
  130.4 0.0 copy-start.1
  130.5 8.9 %maximum_convert_fusion = (f32[1280,1280]{1,0:T(8,128)}, f32[1280,1280]{1,0:T(8,128)}) fusion(bf16[640,1280]{1,0:T(8,128)(2,1)} %bitcast.12, bf16[640,1280]{1,0:T(8,128)(2,1)} %bitcast.11, bf16[1280,640]{1,0:T(8,128)(2,1)} %bitcast.10, bf16[1280,640]{1,0:T(8,128)(2,1)} %bitcast.9), kind=kLoop, calls=%fused_computation | loop fusion | flops 13107200 | bytes 19660800 | tf_op jit(solution)/shard_map/convert_element_type | solution.py:613
  139.4 0.0 copy-done.2
  139.4 0.6 reduce
  140.0 0.0 copy-done
  140.0 0.8 copy.13
  140.8 0.0 copy-done.1
  140.8 0.6 copy.14
Async XLA Ops:
  130.4 8.9 %copy-start.2 = (f32[1,1280]{1,0:T(1,128)S(1)}, f32[1,1280]{1,0:T(1,128)}, u32[]{:S(2)}) copy-start(f32[1,1280]{1,0:T(1,128)} %get-tuple-element.17) | copy-start | bytes 15364
  130.4 9.6 %copy-start = (bf16[192,1280]{1,0:T(8,128)(2,1)S(1)}, bf16[192,1280]{1,0:T(8,128)(2,1)}, u32[]{:S(2)}) copy-start(bf16[192,1280]{1,0:T(8,128)(2,1)} %get-tuple-element.12) | copy-start | bytes 1474564
  130.4 10.3 %copy-start.1 = (f32[7,1280]{1,0:T(8,128)S(1)}, f32[7,1280]{1,0:T(8,128)}, u32[]{:S(2)}) copy-start(f32[7,1280]{1,0:T(8,128)} %get-tuple-element.30) | copy-start | bytes 107524
where the time goes:
time: 142 us; the launch traced here: 141 us
  Pallas kernels  130 us (92%)
  other arithmetic  9.53 us (7%)
    pallas_call x1, Pallas kernels, shards(): pl.pallas_call(functools.partial(body, n, dp_size, rows_in, rows_out, up_...  130 us
    convert_element_type x1, other arithmetic, shards(): jnp.concatenate(rows, axis=0).astype(F32)  8.91 us

commit v1 on v0

v1 whole, which is shorter than its diff:
```python
import functools

import jax
import jax.numpy as jnp
from jax import lax
from jax.experimental import pallas as pl
from jax.experimental.pallas import tpu as pltpu
from jax.sharding import PartitionSpec as P

KW = 7
EDGE = 16
ROWS = 768
FAR = 10
LOOK = 2
VMEM = 45 * 2**20
UP_SHARES = (1,) * 5
MIX_SHARES = (1,) * 5
SUM_SHARES = (1,) * 5
F32 = jnp.float32
BF16 = jnp.bfloat16
MESH = pl.DeviceIdType.MESH


def dot(a, b, dims):
    return lax.dot_general(a, b, (dims, ((), ())), preferred_element_type=F32)


def chunk_of(size):
    return 256 if size % 256 == 0 else size


def scoped(function):
    def wrapped(*args):
        with jax.named_scope(function.__name__ + "".join(f"_{a}" for a in args if isinstance(a, int))):
            return function(*args)

    return wrapped


def cuts(width, unit, shares):
    if width % unit or width // unit < len(shares):
        return [width]
    units = width // unit
    total = sum(shares)
    edges = [units * sum(shares[:i]) // total for i in range(len(shares) + 1)]
    return [(b - a) * unit for a, b in zip(edges, edges[1:])]


def body(
    n, dp_size, up_wide, mix_wide, sum_wide, rows_of,
    x_hbm, h_hbm, up_hbm, win_hbm, wout_hbm, k_ref, gin_ref, gk_ref, gb_ref, *refs,
):
    def take(count):
        nonlocal refs
        got, refs = refs[:count], refs[count:]
        return got

    up_parts, mix_parts, sum_parts = len(up_wide), len(mix_wide), len(sum_wide)
    parts = up_parts + mix_parts
    finals = take(parts)
    accs = take(parts)
    psends = take(parts)
    precvs = take(parts)
    rsends = take(parts)
    rrecvs = take(parts)
    gathers = take(parts)
    sums = take(sum_parts)
    zrecvs = take(sum_parts)
    (
        h_ref, win_ref, wout_ref, act, gh, xpad, gpad, bias, kb, kp, k1, k2, k3,
        ls, hl, ul, hs, hr, us, uf, ur, zs, zr, ps, pr, rs, rr, ds, dr, gs, gr,
        kbs, kbr, kps, kpr, k1s, k1r, k2s, k2r, k3s, k3r,
    ) = refs
    chips = dp_size // 2
    me = lax.axis_index("tp")
    dp = lax.axis_index("dp")
    core = lax.rem(dp, 2)
    chip = dp // 2
    tokens, width = x_hbm.shape
    total_rows, hidden = h_ref.shape
    up_at = [sum(up_wide[:i]) for i in range(up_parts)]
    mix_at = [sum(mix_wide[:i]) for i in range(mix_parts)]
    sum_at = [sum(sum_wide[:i]) for i in range(sum_parts)]
    tall = chunk_of(hidden)
    bits = chips.bit_length() - 1

    def mirror(i):
        return sum((i // 2**p) % 2 * 2 ** (bits - 1 - p) for p in range(bits))

    spots = (chip, mirror(chip))
    halves = [chips >> (s + 1) for s in range(bits)]
    starts = [sum(halves[:s]) for s in range(bits)]

    def span(d, s, other):
        h = halves[s]
        side = lax.rem(spots[d] // h, 2)
        low = spots[d] // h * h
        return low + (h - 2 * h * side if other else 0)

    def peer(d, s):
        h = halves[s]
        spot = spots[d] + h - 2 * h * lax.rem(spots[d] // h, 2)
        return (mirror(spot) if d else spot) * 2 + core

    partner = dp + 1 - 2 * core

    barrier = pltpu.get_barrier_semaphore()
    for j in range(1, n):
        pl.semaphore_signal(
            barrier, inc=1, device_id=(dp, lax.rem(me + j, n)), device_id_type=MESH
        )
    for j in range(1, dp_size):
        pl.semaphore_signal(
            barrier, inc=1, device_id=(lax.rem(dp + j, dp_size), me), device_id_type=MESH
        )
    pl.semaphore_wait(barrier, n - 1 + dp_size - 1)

    def send(src, dst, s, r, to):
        return pltpu.make_async_remote_copy(
            src_ref=src, dst_ref=dst, send_sem=s, recv_sem=r, device_id=to, device_id_type=MESH
        )

    pending = []

    def start(cond, make):
        if cond is None:
            make().start()
        else:

            @pl.when(cond)
            def _():
                make().start()

        pending.append((cond, make))

    ways = (0, 1)
    step_of = (1, -1)
    room = (me, n - 1 - me)
    ahead = (n - 1 - me, me)

    def block_rows(b):
        return pl.ds(pl.multiple_of(b * tokens, tokens), tokens)

    loads = [
        pltpu.make_async_copy(x_hbm, xpad.at[pl.ds(EDGE, tokens)], ls.at[0]),
        pltpu.make_async_copy(wout_hbm, wout_ref, ls.at[1]),
        pltpu.make_async_copy(win_hbm, win_ref, ls.at[2]),
    ]

    def load_hidden(b):
        at = pl.ds(b * tokens, tokens)
        return pltpu.make_async_copy(h_hbm.at[at], h_ref.at[at], hl.at[b])

    def load_up(c):
        src = up_hbm.at[:, pl.ds(up_at[c], up_wide[c])]
        return pltpu.make_async_copy(src, gathers[c].at[block_rows(me)], ul.at[c])

    def place(k, b):
        return gathers[k].at[block_rows(b)]

    def source(k, b, own):
        if own and k < up_parts:
            return up_hbm.at[:, pl.ds(up_at[k], up_wide[k])]
        return place(k, b)

    def chain(k, d, back):
        b = jnp.clip(me - step_of[d] * back, 0, n - 1)
        to = (dp, jnp.clip(me + step_of[d], 0, n - 1))
        return send(source(k, b, back == 0), place(k, b), us.at[k, d, b], ur.at[k, d, b], to)

    def far(k, d):
        to = (dp, jnp.clip(me + 2 * step_of[d], 0, n - 1))
        return send(source(k, me, True), place(k, me), uf.at[k, d], ur.at[k, d, me], to)

    def far_used(k):
        return k < FAR

    def own_send(k, d, cond):
        start(cond & (ahead[d] > 0), functools.partial(chain, k, d, 0))
        if far_used(k):
            start(cond & (room[d] == 0) & (ahead[d] > 1), functools.partial(far, k, d))

    def x_edge(d):
        to = (dp, jnp.clip(me + step_of[d], 0, n - 1))
        src = x_hbm.at[pl.ds(tokens - EDGE if d == 0 else 0, EDGE)]
        dst = xpad.at[pl.ds(0 if d == 0 else EDGE + tokens, EDGE)]
        return send(src, dst, hs.at[d], hr.at[d], to)

    for d in ways:
        start(ahead[d] > 0, functools.partial(x_edge, d))
    for k in range(LOOK):
        for d in ways:
            own_send(k, d, me >= 0)
    for k in range(LOOK, up_parts):
        for d in ways:
            own_send(k, d, room[d] == 0)
    load_hidden(0).start()
    loads[0].start()
    for j in range(1, n):
        load_hidden(j).start()
    for c in range(up_parts):
        load_up(c).start()
    for load in loads[1:]:
        load.start()

    if act.shape[1] > hidden:
        act[:, pl.ds(hidden, act.shape[1] - hidden)] = jnp.zeros(
            (total_rows, act.shape[1] - hidden), BF16
        )
    bias[...] = jnp.zeros_like(bias)

    @pl.when(me == 0)
    def _():
        xpad[pl.ds(0, EDGE), :] = jnp.zeros((EDGE, width), BF16)
        gpad[pl.ds(0, EDGE), :] = jnp.zeros((EDGE, width), BF16)

    @pl.when(me == n - 1)
    def _():
        xpad[pl.ds(EDGE + tokens, EDGE), :] = jnp.zeros((EDGE, width), BF16)
        gpad[pl.ds(EDGE + tokens, EDGE), :] = jnp.zeros((EDGE, width), BF16)

    @scoped
    def gelu(b):
        load_hidden(b).wait()

        def gelu_step(i, _):
            at = pl.ds(pl.multiple_of(b * tokens + i * 32, 32), 32)
            v = h_ref[at, :].astype(F32)
            cdf = 0.5 + 0.5 * lax.erf(v * 0.7071067811865476)
            act[at, pl.ds(0, hidden)] = (v * cdf).astype(BF16)
            gh[at, :] = (cdf + v * (0.3989422804014327 * jnp.exp(-0.5 * v * v))).astype(BF16)
            return 0

        lax.fori_loop(0, tokens // 32, gelu_step, 0)

    @scoped
    def mix():
        for c in range(mix_parts):

            def mix_step(i, _, c=c):
                lane = pl.ds(pl.multiple_of(i * 128, 128), 128)
                at = pl.ds(pl.multiple_of(mix_at[c] + i * 128, 128), 128)
                x = xpad[:, at].astype(F32)
                taps = k_ref[:, at]
                total = x[EDGE : EDGE + tokens]
                for tap in range(KW):
                    low = EDGE - 3 + tap
                    total = total + taps[tap : tap + 1] * x[low : low + tokens]
                gathers[up_parts + c][block_rows(me), lane] = total.astype(BF16)
                return 0

            lax.fori_loop(0, mix_wide[c] // 128, mix_step, 0)

    @scoped
    def grad_dot(w):
        if w < up_parts:
            left, right = act, gathers[w]
        else:
            left, right = gathers[w], gh
        high = 2 * chips * rows_of[w]
        for half in (1 - core, core):
            lane = pl.ds(pl.multiple_of(half * high, 128), high)
            value = dot(left[:, lane], right[...], ((0,), (0,)))
            if half is core:
                accs[w][...] = value
            else:
                psends[w][...] = value.astype(BF16)
                start(None, functools.partial(pair_copy, w))

    group = tokens * max(g for g in range(1, n + 1) if n % g == 0 and tokens * g <= ROWS)

    @scoped
    def back_dot():
        def back_step(i, _):
            at = pl.ds(pl.multiple_of(i * tall, tall), tall) if tall < hidden else pl.ds(0, hidden)

            def group_step(g, _):
                row = pl.ds(pl.multiple_of(g * group, group), group)
                back = None
                for c in range(up_parts):
                    term = dot(
                        gathers[c][row, :], wout_ref[at, pl.ds(up_at[c], up_wide[c])], ((1,), (1,))
                    )
                    back = term if back is None else back + term
                grad = (gh[row, at].astype(F32) * back).astype(BF16)
                gh[row, at] = grad
                bias[:, at] += jnp.sum(grad.astype(F32), axis=0, keepdims=True)
                return 0

            if group == total_rows:
                group_step(0, 0)
            else:
                lax.fori_loop(0, total_rows // group, group_step, 0)
            return 0

        lax.fori_loop(0, hidden // tall, back_step, 0)

    @scoped
    def part_dot(r):
        wide = chunk_of(sum_wide[r])

        def part_step(i, _):
            lane = pl.ds(pl.multiple_of(i * wide, wide), wide)
            at = pl.ds(pl.multiple_of(sum_at[r] + i * wide, wide), wide)

            def group_step(g, _):
                row = pl.ds(pl.multiple_of(g * group, group), group)
                sums[r][row, lane] = dot(gh[row, :], win_ref[at, :], ((1,), (1,))).astype(BF16)
                return 0

            if group == total_rows:
                group_step(0, 0)
            else:
                lax.fori_loop(0, total_rows // group, group_step, 0)
            return 0

        lax.fori_loop(0, sum_wide[r] // wide, part_step, 0)

    def rows_at(w, d, block):
        return pl.ds(pl.multiple_of((d * chips + block) * rows_of[w], 8), rows_of[w])

    def pair_copy(w):
        return send(psends[w], precvs[w], ps.at[w], pr.at[w], (partner, me))

    def own(w, d, block):
        at = rows_at(w, d, block)
        return accs[w][at, :] + precvs[w][at, :].astype(F32)

    def ring_reduce(w, d, s):
        at = pl.ds(starts[s], halves[s])
        return send(
            rsends[w].at[d, at], rrecvs[w].at[d, at], rs.at[w, d, s], rr.at[w, d, s],
            (peer(d, s), me),
        )

    def ring_gather(w, d, s, other):
        ref = finals[w].at[core, d, pl.ds(span(d, s, other), halves[s])]
        at = 2 * bits - 1 - s
        return send(ref, ref, rs.at[w, d, at], rr.at[w, d, at], (peer(d, s), me))

    def across(w, d, s, half):
        if s == bits:
            ref = finals[w].at[half, d, pl.ds(spots[d], 1)]
        else:
            ref = finals[w].at[half, d, pl.ds(span(d, s, True), halves[s])]
        return send(ref, ref, ds.at[w, d, s], dr.at[w, d, s], (partner, me))

    last = 2 * bits

    @scoped
    def ring_step(w, s):
        acc, rsend, rrecv, final = accs[w], rsends[w], rrecvs[w], finals[w]
        if s == 0:
            pair_copy(w).wait_recv()
        for d in ways:
            if s <= bits:
                if s > 0:
                    ring_reduce(w, d, s - 1).wait_recv()

                def value(block, s=s, d=d):
                    if s == 0:
                        return own(w, d, block)
                    got = rrecv[d, starts[s - 1] + block - span(d, s - 1, False)].astype(F32)
                    if s == 1:
                        return own(w, d, block) + got
                    return acc[rows_at(w, d, block), :] + got

                if s == bits:
                    final[core, d, spots[d]] = value(spots[d]).astype(BF16)
                    start(None, functools.partial(ring_gather, w, d, s - 1, False))
                    start(None, functools.partial(across, w, d, bits, core))
                    continue
                for j in range(halves[s]):
                    rsend[d, starts[s] + j] = value(span(d, s, True) + j).astype(BF16)
                start(None, functools.partial(ring_reduce, w, d, s))
                if s > 0:
                    for j in range(halves[s]):
                        block = span(d, s, False) + j
                        acc[rows_at(w, d, block), :] = value(block)
            else:
                step = 2 * bits - s
                ring_gather(w, d, step, True).wait_recv()
                if step > 0:
                    start(None, functools.partial(ring_gather, w, d, step - 1, False))
                start(None, functools.partial(across, w, d, step, core))

    @scoped
    def ring_end(w):
        for d in ways:
            for s in range(bits + 1):
                across(w, d, s, 1 - core).wait_recv()

    def target(d, t, behind):
        place = room[d] - behind
        block = n - 1 - t + place
        return block if d == 0 else n - 1 - block

    def z_slot(d, block, owner):
        return jnp.where((block == owner) & (d == 1), n, block)

    def z_send(r, d, t):
        block = jnp.clip(target(d, t, 0), 0, n - 1)
        to = jnp.clip(me + step_of[d], 0, n - 1)
        return send(
            sums[r].at[block_rows(block)], zrecvs[r].at[z_slot(d, block, to)],
            zs.at[r, d, t], zr.at[r, d, t], (dp, to),
        )

    def z_arrive(r, d, t):
        block = jnp.clip(target(d, t, 1), 0, n - 1)
        slot = zrecvs[r].at[z_slot(d, block, me)]
        return send(slot, slot, zs.at[r, d, t], zr.at[r, d, t], (dp, jnp.clip(me + 1, 0, n - 1)))

    @scoped
    def z_step(r, t):
        for d in ways:
            if t > 0:

                @pl.when((room[d] >= 1) & (room[d] - 1 <= t - 1))
                def _(d=d):
                    z_arrive(r, d, t - 1).wait_recv()
                    if t < n - 1:
                        block = jnp.clip(target(d, t - 1, 1), 0, n - 1)
                        at = block_rows(block)
                        sums[r][at, :] = (
                            sums[r][at, :].astype(F32) + zrecvs[r][z_slot(d, block, me)].astype(F32)
                        ).astype(BF16)

            if t < n - 1:
                start(
                    (room[d] <= t) & (room[d] > 0) & (ahead[d] > 0),
                    functools.partial(z_send, r, d, t),
                )

    def z_first(r):
        for t in range(n - 1):
            for d in ways:
                start((room[d] == 0) & (ahead[d] > 0), functools.partial(z_send, r, d, t))

    active = []

    def tick(count=1):
        for _ in range(count):
            for item in list(active):
                ring_step(item[0], item[1])
                item[1] += 1
                if item[1] > last:
                    active.remove(item)

    def relays(k, d, back):
        go = (room[d] >= back) & (ahead[d] > 0)
        return go & (room[d] > 1) if far_used(k) and back == 1 else go

    @scoped
    def forward(k):
        for back in range(1, n):
            for d in ways:
                if back < n - 1:

                    @pl.when(relays(k, d, back))
                    def _(d=d):
                        chain(k, d, back).wait_recv()

                    start(relays(k, d, back), functools.partial(chain, k, d, back))
                if k + LOOK < parts:
                    own_send(k + LOOK, d, room[d] == back)

    @scoped
    def arrive(k):
        for back in range(1, n):
            for d in ways:

                @pl.when((room[d] >= back) & jnp.logical_not(relays(k, d, back)))
                def _(d=d):
                    chain(k, d, back).wait_recv()

    gelu(0)
    loads[0].wait()
    for d in ways:

        @pl.when(room[d] > 0)
        def _(d=d):
            x_edge(d).wait_recv()

    mix()
    for k in range(up_parts, parts):
        for d in ways:
            own_send(k, d, room[d] == 0)
    for b in range(1, n):
        gelu(b)
    for c in range(up_parts):
        load_up(c).wait()

    def bias_send(j):
        to = lax.rem(dp + j, dp_size)
        return send(kb.at[dp], kb.at[dp], kbs.at[j], kbr.at[dp], (to, me))

    def bias_arrive(j):
        src = lax.rem(dp + j, dp_size)
        return send(kb.at[src], kb.at[src], kbs.at[j], kbr.at[src], (src, me))

    sent = 0

    def relay_to(k):
        nonlocal sent
        while sent < min(k, parts):
            forward(sent)
            sent += 1

    def grad(k):
        arrive(k)
        grad_dot(k)
        tick()
        active.append([k, 1])
        ring_step(k, 0)

    for k in range(up_parts):
        relay_to(k + 1)
        if k == up_parts - 1:
            loads[1].wait()
            loads[2].wait()
        grad(k)
    relay_to(up_parts + 2)
    back_dot()
    kb[dp] = bias[...]
    for j in range(1, dp_size):
        start(None, functools.partial(bias_send, j))
    for r in range(sum_parts):
        part_dot(r)
        z_first(r)
    relay_to(parts)
    summed = 0
    for k in range(up_parts, parts):
        grad(k)
        while summed < sum_parts and summed < (k - up_parts):
            for t in range(1, n - 1):
                z_step(summed, t)
            summed += 1
    while summed < sum_parts:
        for t in range(1, n - 1):
            z_step(summed, t)
        summed += 1
    tick()
    for r in range(sum_parts):
        z_step(r, n - 1)

    @scoped
    def total_grad():
        edges = sorted(set(up_at + sum_at + [width]))
        for low, top in zip(edges, edges[1:]):
            c = max(i for i in range(up_parts) if up_at[i] <= low)
            r = max(i for i in range(sum_parts) if sum_at[i] <= low)

            def sum_step(i, _, low=low, c=c, r=r):
                at = pl.ds(pl.multiple_of(low + i * 128, 128), 128)
                lane = pl.ds(pl.multiple_of(low - sum_at[r] + i * 128, 128), 128)
                up_lane = pl.ds(pl.multiple_of(low - up_at[c] + i * 128, 128), 128)
                up = gathers[c][block_rows(me), up_lane].astype(F32)
                mine = sums[r][block_rows(me), lane].astype(F32)
                left = jnp.where(me > 0, zrecvs[r][me, :, lane].astype(F32), 0.0)
                right = jnp.where(me < n - 1, zrecvs[r][n, :, lane].astype(F32), 0.0)
                gpad[pl.ds(EDGE, tokens), at] = (up + (mine + left + right)).astype(BF16)
                return 0

            lax.fori_loop(0, (top - low) // 128, sum_step, 0)

    total_grad()

    def g_edge(d):
        to = (dp, jnp.clip(me + step_of[d], 0, n - 1))
        src = gpad.at[pl.ds(tokens if d == 0 else EDGE, EDGE)]
        dst = gpad.at[pl.ds(0 if d == 0 else EDGE + tokens, EDGE)]
        return send(src, dst, gs.at[d], gr.at[d], to)

    for d in ways:
        start(ahead[d] > 0, functools.partial(g_edge, d))

    @scoped
    def taps():
        def taps_step(i, _):
            at = pl.ds(pl.multiple_of(i * 128, 128), 128)
            g = gpad[pl.ds(EDGE, tokens), at].astype(F32)
            x = xpad[:, at].astype(F32)
            sums = [
                jnp.sum(g * x[EDGE - 3 + tap : EDGE - 3 + tap + tokens], axis=0, keepdims=True)
                for tap in range(KW)
            ]
            sums.append(jnp.zeros_like(sums[0]))
            kp[i // (width // 256), :, pl.ds(pl.multiple_of(lax.rem(i, width // 256) * 128, 128), 128)] = jnp.concatenate(sums, axis=0)
            return 0

        lax.fori_loop(0, width // 128, taps_step, 0)

    taps()

    def pair_taps():
        return send(kp.at[1 - core], kp.at[2], kps.at[0], kpr.at[0], (partner, me))

    start(None, pair_taps)
    tick()

    def k1_send(j):
        to = lax.rem(me + j, n)
        return send(k1.at[me], k1.at[me], k1s.at[j], k1r.at[me], (dp, to))

    def k1_arrive(j):
        src = lax.rem(me + j, n)
        return send(k1.at[src], k1.at[src], k1s.at[j], k1r.at[src], (dp, src))

    pair_taps().wait_recv()
    k1[me] = kp[core] + kp[2]
    for j in range(1, n):
        start(None, functools.partial(k1_send, j))
    for d in ways:

        @pl.when(room[d] > 0)
        def _(d=d):
            g_edge(d).wait_recv()

    @scoped
    def gin():
        def gin_step(i, _):
            at = pl.ds(pl.multiple_of(i * 128, 128), 128)
            g = gpad[:, at].astype(F32)
            taps = k_ref[:, at]
            total = g[EDGE : EDGE + tokens]
            for tap in range(KW):
                low = EDGE + 3 - tap
                total = total + taps[tap : tap + 1] * g[low : low + tokens]
            gin_ref[:, at] = total.astype(BF16)
            return 0

        lax.fori_loop(0, width // 128, gin_step, 0)

    gin()
    tick()

    @scoped
    def k1_wait():
        for j in range(1, n):
            k1_arrive(j).wait_recv()

    k1_wait()
    taps_sum = k1[0]
    for j in range(1, n):
        taps_sum = taps_sum + k1[j]
    k2[chip] = taps_sum

    def k2_send(j):
        to = lax.rem(chip + j, chips) * 2 + core
        return send(k2.at[chip], k2.at[chip], k2s.at[j], k2r.at[chip], (to, me))

    def k2_arrive(j):
        src = lax.rem(chip + j, chips)
        return send(k2.at[src], k2.at[src], k2s.at[j], k2r.at[src], (src * 2 + core, me))

    for j in range(1, chips):
        start(None, functools.partial(k2_send, j))
    tick()

    @scoped
    def k2_wait():
        for j in range(1, chips):
            k2_arrive(j).wait_recv()

    k2_wait()
    total = k2[0]
    for j in range(1, chips):
        total = total + k2[j]
    k3[core] = total

    def k3_copy(half):
        return send(k3.at[half], k3.at[half], k3s.at[0], k3r.at[0], (partner, me))

    start(None, functools.partial(k3_copy, core))
    while active:
        tick()
    for j in range(1, dp_size):
        bias_arrive(j).wait_recv()
    total = kb[0]
    for j in range(1, dp_size):
        total = total + kb[j]
    gb_ref[...] = total
    k3_copy(1 - core).wait_recv()
    for half in range(2):
        gk_ref[:, pl.ds(half * (width // 2), width // 2)] = k3[half, :KW]
    for w in range(parts):
        ring_end(w)

    @scoped
    def drain():
        for cond, make in pending:
            if cond is None:
                make().wait_send()
            else:

                @pl.when(cond)
                def _(make=make):
                    make().wait_send()

    drain()


def shards(n, dp_size, inputs, saved_hidden, upstream, w_in, w_out, kernel):
    chips = dp_size // 2
    tokens, width = inputs.shape[1:]
    hidden = w_in.shape[1]
    total_rows = n * tokens
    up_wide = cuts(width, 256, UP_SHARES)
    mix_wide = cuts(width, 64 * chips, MIX_SHARES)
    sum_wide = cuts(width, 256, SUM_SHARES)
    up_parts, mix_parts, sum_parts = len(up_wide), len(mix_wide), len(sum_wide)
    parts = up_parts + mix_parts
    rows_out = -(-hidden // (4 * chips * 8)) * 8
    high = rows_out * 4 * chips
    rows_of = [rows_out] * up_parts + [wide // (4 * chips) for wide in mix_wide]
    sizes = [(rows_out, wide) for wide in up_wide] + [
        (rows, hidden) for rows in rows_of[up_parts:]
    ]
    dma = pltpu.SemaphoreType.DMA
    bits = chips.bit_length() - 1
    vmem = pl.BlockSpec(memory_space=pltpu.VMEM)
    hbm = pl.BlockSpec(memory_space=pltpu.HBM)
    shape = jax.ShapeDtypeStruct
    grad_inputs, grad_kernel, grad_bias, *finals = pl.pallas_call(
        functools.partial(body, n, dp_size, up_wide, mix_wide, sum_wide, rows_of),
        out_shape=[shape((tokens, width), BF16), shape((KW, width), F32), shape((1, hidden), F32)]
        + [shape((2, 2, chips) + size, BF16) for size in sizes],
        in_specs=[hbm] * 5 + [vmem],
        out_specs=[vmem] * (3 + parts),
        scratch_shapes=[pltpu.VMEM((2 * chips * r, c), F32) for r, c in sizes]
        + [pltpu.VMEM((2 * chips * r, c), BF16) for r, c in sizes] * 2
        + [pltpu.VMEM((2, chips - 1) + size, BF16) for size in sizes] * 2
        + [pltpu.VMEM((total_rows, wide), BF16) for wide in up_wide + mix_wide]
        + [pltpu.VMEM((total_rows, wide), BF16) for wide in sum_wide]
        + [pltpu.VMEM((n + 1, tokens, wide), BF16) for wide in sum_wide]
        + [
            pltpu.VMEM((total_rows, hidden), BF16),
            pltpu.VMEM((width, hidden), BF16),
            pltpu.VMEM((hidden, width), BF16),
            pltpu.VMEM((total_rows, high), BF16),
            pltpu.VMEM((total_rows, hidden), BF16),
            pltpu.VMEM((tokens + 2 * EDGE, width), BF16),
            pltpu.VMEM((tokens + 2 * EDGE, width), BF16),
            pltpu.VMEM((1, hidden), F32),
            pltpu.VMEM((dp_size, 1, hidden), F32),
            pltpu.VMEM((3, 8, width // 2), F32),
            pltpu.VMEM((n, 8, width // 2), F32),
            pltpu.VMEM((chips, 8, width // 2), F32),
            pltpu.VMEM((2, 8, width // 2), F32),
            dma((3,)), dma((n,)), dma((up_parts,)),
            dma((2,)), dma((2,)),
            dma((parts, 2, n)), dma((parts, 2)), dma((parts, 2, n)),
            dma((sum_parts, 2, n)), dma((sum_parts, 2, n)),
            dma((parts,)), dma((parts,)),
            dma((parts, 2, 2 * bits)), dma((parts, 2, 2 * bits)),
            dma((parts, 2, bits + 1)), dma((parts, 2, bits + 1)),
            dma((2,)), dma((2,)),
            dma((dp_size,)), dma((dp_size,)),
            dma((1,)), dma((1,)),
            dma((n,)), dma((n,)),
            dma((chips,)), dma((chips,)),
            dma((1,)), dma((1,)),
        ],
        compiler_params=pltpu.CompilerParams(
            collective_id=0, has_side_effects=True, vmem_limit_bytes=VMEM if total_rows <= ROWS else 67043328
        ),
    )(
        inputs[0],
        saved_hidden[0],
        upstream[0],
        w_in,
        w_out,
        kernel,
    )
    outs = [f.reshape(high, wide) for f, wide in zip(finals, up_wide)]
    outs += [f.reshape(wide, hidden) for f, wide in zip(finals[up_parts:], mix_wide)]
    return tuple(
        pl.pallas_call(
            functools.partial(widen, up_wide, mix_wide),
            out_shape=[
                shape((1, tokens, width), BF16),
                shape((width, hidden), F32),
                shape((hidden, width), F32),
                shape((hidden,), F32),
                shape((KW, width), F32),
            ],
            in_specs=[vmem] * (parts + 3),
            out_specs=[hbm] * 3 + [vmem] + [hbm],
            scratch_shapes=[pltpu.VMEM((wide, hidden), F32) for wide in mix_wide]
            + [pltpu.VMEM((hidden, wide), F32) for wide in up_wide]
            + [dma((parts + 2,))],
            compiler_params=pltpu.CompilerParams(vmem_limit_bytes=24 * 2**20),
        )(*outs, grad_inputs, grad_kernel, grad_bias)
    )


def widen(up_wide, mix_wide, *refs):
    up_parts, mix_parts = len(up_wide), len(mix_wide)
    parts = up_parts + mix_parts
    finals, (gin, gk, gb), refs = refs[:parts], refs[parts : parts + 3], refs[parts + 3 :]
    gin_out, rows_out, cols_out, gb_out, gk_out, *refs = refs
    rows, cols, sem = refs[:mix_parts], refs[mix_parts:-1], refs[-1]
    copies = [
        pltpu.make_async_copy(gin, gin_out.at[0], sem.at[parts]),
        pltpu.make_async_copy(gk, gk_out, sem.at[parts + 1]),
    ]
    for copy in copies:
        copy.start()
    gb_out[...] = gb[0]

    def widen_one(source, target):
        high = target.shape[0]
        step = 64

        def widen_step(i, _):
            at = pl.ds(pl.multiple_of(i * step, step), step)
            target[at, :] = source[at, :].astype(F32)
            return 0

        lax.fori_loop(0, high // step, widen_step, 0)

    for c in range(mix_parts):
        widen_one(finals[up_parts + c], rows[c])
        at = pl.ds(sum(mix_wide[:c]), mix_wide[c])
        copies.append(pltpu.make_async_copy(rows[c], rows_out.at[at], sem.at[c]))
        copies[-1].start()
    for c in range(up_parts):
        widen_one(finals[c], cols[c])
        at = pl.ds(sum(up_wide[:c]), up_wide[c])
        copies.append(pltpu.make_async_copy(cols[c], cols_out.at[:, at], sem.at[mix_parts + c]))
        copies[-1].start()
    for copy in copies:
        copy.wait()


def solution(mesh):
    in_specs = (
        P("dp", "tp", None),
        P("dp", None, "tp"),
        P("dp", "tp", None),
        P(None, "tp"),
        P("tp", None),
        P(),
    )
    out_specs = (P("dp", "tp", None), P(None, "tp"), P("tp", None), P("tp"), P())
    return jax.shard_map(
        functools.partial(shards, mesh.shape["tp"], mesh.shape["dp"]),
        mesh=mesh,
        in_specs=in_specs,
        out_specs=out_specs,
        check_vma=False,
    )
```

time: 142 us -> 121 us (0.85)
  Pallas kernels: 130 us -> 117 us
  other arithmetic: 9.53 us -> 0 us
  local copies, waits for them, and re-layouts: 1.41 us -> 2.83 us
    pallas_call x1 -> x2, Pallas kernels: 130 us -> 117 us  [the longest x1 112 us: shards(): pl.pallas_call(functools.partial(body, n, dp_size, up_wide, mix_wide, sum...]
    convert_element_type x1 -> x0, other arithmetic: 8.91 us -> none  [shards(): jnp.concatenate(rows, axis=0).astype(F32)]
    unnamed x8 -> x6, local copies, waits for them, and re-layouts: 1.41 us -> 2.83 us
where the time goes in v1:
time: 121 us
  Pallas kernels  117 us (97%)
  local copies, waits for them, and re-layouts  2.83 us (2%)
    pallas_call x1, Pallas kernels, shards(): pl.pallas_call(functools.partial(body, n, dp_size, up_wide, mix_wide, sum...  112 us
    pallas_call x1, Pallas kernels, shards(): pl.pallas_call(functools.partial(widen, up_wide, mix_wide), out_shape=[sh...  5.59 us
    unnamed x6, local copies, waits for them, and re-layouts  2.83 us

profile of v1, /device:TPU:1, one launch (start us, length us, event | category | flops | bytes accessed | tf_op | source)
XLA Modules:
  0.0 120.8 jit_solution(1639563380885195418)
XLA Ops:
  0.6 0.0 copy-start
  0.6 1.0 copy-done
  1.7 0.0 copy-start.1
  1.7 1.0 copy-done.1
  2.7 0.0 copy-start.2
  2.7 0.8 copy-done.2
  3.5 111.5 %shard_map.101 = (bf16[192,1280]{1,0:T(8,128)(2,1)S(1)}, f32[7,1280]{1,0:T(8,128)S(1)}, f32[1,1280]{1,0:T(1,128)S(1)}, bf16[2,2,4,80,256]{4,3,2,1,0:T(8,128)(2,1...) custom-call(bf16[192,1280]{1,0:T(8,128)(2,1)S(1)} %bitcast.23, ...), custom_call_target="tpu_custom_call" | custom-call | tf_op jit(solution)/shard_map/pallas_call | solution.py:725
  115.0 5.6 %shard_map.102 = (bf16[1,192,1280]{2,1,0:T(8,128)(2,1)}, f32[1280,1280]{1,0:T(8,128)}, f32[1280,1280]{1,0:T(8,128)}, f32[1280]{0:T(1024)}, f32[7,1280]{1,0:T(8,128)}) custom-call(bf16[1280,256]{1,0:T(8,128)(2,1)S(1)} %bitcast.13, bf16[1280,256]{1,0:T(8,128)(2,1)S(1)} %bitcast.14, bf16[1280,256]{1,0:T(8,128)(2,1)S(1)} %bitcast.15, ...), custom_call_target="tpu_custom_call" | custom-call | tf_op jit(solution)/shard_map/pallas_call | solution.py:779
Async XLA Ops:
  0.6 1.0 copy-start
  1.7 1.0 copy-start.1
  2.7 0.8 copy-start.2

commit v2 on v1

--- a/solution.py
+++ b/solution.py
@@ -68,7 +68,7 @@
     zrecvs = take(sum_parts)
     (
         h_ref, win_ref, wout_ref, act, gh, xpad, gpad, bias, kb, kp, k1, k2, k3,
-        ls, hl, ul, hs, hr, us, uf, ur, zs, zr, ps, pr, rs, rr, ds, dr, gs, gr,
+        ls, hl, ul, hs, hr, us, ur, zs, zr, ps, pr, rs, rr, ds, dr, gs, gr,
         kbs, kbr, kps, kpr, k1s, k1r, k2s, k2r, k3s, k3r,
     ) = refs
     chips = dp_size // 2
@@ -122,7 +122,7 @@
 
     pending = []
 
-    def start(cond, make):
+    def start(cond, make, keep=True):
         if cond is None:
             make().start()
         else:
@@ -131,7 +131,11 @@
             def _():
                 make().start()
 
-        pending.append((cond, make))
+        if keep:
+            pending.append((cond, make))
+
+    def group(ref, s, r):
+        return send(ref, ref, s, r, (partner, me))
 
     ways = (0, 1)
     step_of = (1, -1)
@@ -166,19 +170,39 @@
     def chain(k, d, back):
         b = jnp.clip(me - step_of[d] * back, 0, n - 1)
         to = (dp, jnp.clip(me + step_of[d], 0, n - 1))
-        return send(source(k, b, back == 0), place(k, b), us.at[k, d, b], ur.at[k, d, b], to)
+        return send(source(k, b, back == 0), place(k, b), us.at[k, d], ur.at[k, b], to)
 
     def far(k, d):
         to = (dp, jnp.clip(me + 2 * step_of[d], 0, n - 1))
-        return send(source(k, me, True), place(k, me), uf.at[k, d], ur.at[k, d, me], to)
+        return send(source(k, me, True), place(k, me), us.at[k, d], ur.at[k, me], to)
 
     def far_used(k):
         return k < FAR
 
     def own_send(k, d, cond):
-        start(cond & (ahead[d] > 0), functools.partial(chain, k, d, 0))
+        start(cond & (ahead[d] > 0), functools.partial(chain, k, d, 0), False)
         if far_used(k):
-            start(cond & (room[d] == 0) & (ahead[d] > 1), functools.partial(far, k, d))
+            start(cond & (room[d] == 0) & (ahead[d] > 1), functools.partial(far, k, d), False)
+
+    def free(k):
+        return 1 if far_used(k) else 0
+
+    def later(k):
+        if k == up_parts - 1:
+            return range(up_parts, min(up_parts + LOOK, parts))
+        if k + LOOK < up_parts or up_parts <= k < parts - LOOK:
+            return [k + LOOK]
+        return []
+
+    def sent_of(m, k, d):
+        front, behind = (n - 1 - m, m) if d == 0 else (m, n - 1 - m)
+        if front == 0:
+            return 0
+        count = 1 + (far_used(k) and behind == 0 and front > 1)
+        return count + sum(
+            behind >= back and not (far_used(k) and back == 1 and behind == 1)
+            for back in range(1, n - 1)
+        )
 
     def x_edge(d):
         to = (dp, jnp.clip(me + step_of[d], 0, n - 1))
@@ -193,7 +217,7 @@
             own_send(k, d, me >= 0)
     for k in range(LOOK, up_parts):
         for d in ways:
-            own_send(k, d, room[d] == 0)
+            own_send(k, d, room[d] <= free(k))
     load_hidden(0).start()
     loads[0].start()
     for j in range(1, n):
@@ -267,7 +291,7 @@
                 psends[w][...] = value.astype(BF16)
                 start(None, functools.partial(pair_copy, w))
 
-    group = tokens * max(g for g in range(1, n + 1) if n % g == 0 and tokens * g <= ROWS)
+    batch = tokens * max(g for g in range(1, n + 1) if n % g == 0 and tokens * g <= ROWS)
 
     @scoped
     def back_dot():
@@ -275,7 +299,7 @@
             at = pl.ds(pl.multiple_of(i * tall, tall), tall) if tall < hidden else pl.ds(0, hidden)
 
             def group_step(g, _):
-                row = pl.ds(pl.multiple_of(g * group, group), group)
+                row = pl.ds(pl.multiple_of(g * batch, batch), batch)
                 back = None
                 for c in range(up_parts):
                     term = dot(
@@ -287,34 +311,30 @@
                 bias[:, at] += jnp.sum(grad.astype(F32), axis=0, keepdims=True)
                 return 0
 
-            if group == total_rows:
+            if batch == total_rows:
                 group_step(0, 0)
             else:
-                lax.fori_loop(0, total_rows // group, group_step, 0)
+                lax.fori_loop(0, total_rows // batch, group_step, 0)
             return 0
 
         lax.fori_loop(0, hidden // tall, back_step, 0)
 
     @scoped
-    def part_dot(r):
-        wide = chunk_of(sum_wide[r])
-
-        def part_step(i, _):
-            lane = pl.ds(pl.multiple_of(i * wide, wide), wide)
-            at = pl.ds(pl.multiple_of(sum_at[r] + i * wide, wide), wide)
-
-            def group_step(g, _):
-                row = pl.ds(pl.multiple_of(g * group, group), group)
-                sums[r][row, lane] = dot(gh[row, :], win_ref[at, :], ((1,), (1,))).astype(BF16)
-                return 0
-
-            if group == total_rows:
-                group_step(0, 0)
-            else:
-                lax.fori_loop(0, total_rows // group, group_step, 0)
+    def part_dot(r, count):
+        at = pl.ds(sum_at[r], sum(sum_wide[r : r + count]))
+
+        def group_step(g, _):
+            row = pl.ds(pl.multiple_of(g * batch, batch), batch)
+            value = dot(gh[row, :], win_ref[at, :], ((1,), (1,))).astype(BF16)
+            for j in range(r, r + count):
+                low = sum_at[j] - sum_at[r]
+                sums[j][row, :] = value[:, low : low + sum_wide[j]]
             return 0
 
-        lax.fori_loop(0, sum_wide[r] // wide, part_step, 0)
+        if batch == total_rows:
+            group_step(0, 0)
+        else:
+            lax.fori_loop(0, total_rows // batch, group_step, 0)
 
     def rows_at(w, d, block):
         return pl.ds(pl.multiple_of((d * chips + block) * rows_of[w], 8), rows_of[w])
@@ -329,21 +349,21 @@
     def ring_reduce(w, d, s):
         at = pl.ds(starts[s], halves[s])
         return send(
-            rsends[w].at[d, at], rrecvs[w].at[d, at], rs.at[w, d, s], rr.at[w, d, s],
+            rsends[w].at[d, at], rrecvs[w].at[d, at], rs.at[w], rr.at[w, s],
             (peer(d, s), me),
         )
 
     def ring_gather(w, d, s, other):
         ref = finals[w].at[core, d, pl.ds(span(d, s, other), halves[s])]
         at = 2 * bits - 1 - s
-        return send(ref, ref, rs.at[w, d, at], rr.at[w, d, at], (peer(d, s), me))
+        return send(ref, ref, rs.at[w], rr.at[w, at], (peer(d, s), me))
 
     def across(w, d, s, half):
         if s == bits:
             ref = finals[w].at[half, d, pl.ds(spots[d], 1)]
         else:
             ref = finals[w].at[half, d, pl.ds(span(d, s, True), halves[s])]
-        return send(ref, ref, ds.at[w, d, s], dr.at[w, d, s], (partner, me))
+        return send(ref, ref, ds.at[w], dr.at[w], (partner, me))
 
     last = 2 * bits
 
@@ -352,10 +372,12 @@
         acc, rsend, rrecv, final = accs[w], rsends[w], rrecvs[w], finals[w]
         if s == 0:
             pair_copy(w).wait_recv()
+        else:
+            j = s - 1 if s <= bits else 2 * bits - s
+            both = rrecv.at[:, pl.ds(starts[j], halves[j])]
+            group(both, rs.at[w], rr.at[w, s - 1]).wait_recv()
         for d in ways:
             if s <= bits:
-                if s > 0:
-                    ring_reduce(w, d, s - 1).wait_recv()
 
                 def value(block, s=s, d=d):
                     if s == 0:
@@ -367,28 +389,25 @@
 
                 if s == bits:
                     final[core, d, spots[d]] = value(spots[d]).astype(BF16)
-                    start(None, functools.partial(ring_gather, w, d, s - 1, False))
-                    start(None, functools.partial(across, w, d, bits, core))
+                    start(None, functools.partial(ring_gather, w, d, s - 1, False), False)
+                    start(None, functools.partial(across, w, d, bits, core), False)
                     continue
                 for j in range(halves[s]):
                     rsend[d, starts[s] + j] = value(span(d, s, True) + j).astype(BF16)
-                start(None, functools.partial(ring_reduce, w, d, s))
+                start(None, functools.partial(ring_reduce, w, d, s), False)
                 if s > 0:
                     for j in range(halves[s]):
                         block = span(d, s, False) + j
                         acc[rows_at(w, d, block), :] = value(block)
             else:
                 step = 2 * bits - s
-                ring_gather(w, d, step, True).wait_recv()
                 if step > 0:
-                    start(None, functools.partial(ring_gather, w, d, step - 1, False))
-                start(None, functools.partial(across, w, d, step, core))
+                    start(None, functools.partial(ring_gather, w, d, step - 1, False), False)
+                start(None, functools.partial(across, w, d, step, core), False)
 
     @scoped
     def ring_end(w):
-        for d in ways:
-            for s in range(bits + 1):
-                across(w, d, s, 1 - core).wait_recv()
+        group(finals[w].at[1 - core], ds.at[w], dr.at[w]).wait_recv()
 
     def target(d, t, behind):
         place = room[d] - behind
@@ -403,13 +422,13 @@
         to = jnp.clip(me + step_of[d], 0, n - 1)
         return send(
             sums[r].at[block_rows(block)], zrecvs[r].at[z_slot(d, block, to)],
-            zs.at[r, d, t], zr.at[r, d, t], (dp, to),
+            zs.at[r], zr.at[r, z_slot(d, block, to)], (dp, to),
         )
 
     def z_arrive(r, d, t):
         block = jnp.clip(target(d, t, 1), 0, n - 1)
-        slot = zrecvs[r].at[z_slot(d, block, me)]
-        return send(slot, slot, zs.at[r, d, t], zr.at[r, d, t], (dp, jnp.clip(me + 1, 0, n - 1)))
+        slot = z_slot(d, block, me)
+        return group(zrecvs[r].at[slot], zs.at[r], zr.at[r, slot])
 
     @scoped
     def z_step(r, t):
@@ -430,12 +449,12 @@
                 start(
                     (room[d] <= t) & (room[d] > 0) & (ahead[d] > 0),
                     functools.partial(z_send, r, d, t),
+                    False,
                 )
 
-    def z_first(r):
-        for t in range(n - 1):
-            for d in ways:
-                start((room[d] == 0) & (ahead[d] > 0), functools.partial(z_send, r, d, t))
+    def z_first(r, t):
+        for d in ways:
+            start((room[d] == 0) & (ahead[d] > 0), functools.partial(z_send, r, d, t), False)
 
     active = []
 
@@ -461,9 +480,9 @@
                     def _(d=d):
                         chain(k, d, back).wait_recv()
 
-                    start(relays(k, d, back), functools.partial(chain, k, d, back))
-                if k + LOOK < parts:
-                    own_send(k + LOOK, d, room[d] == back)
+                    start(relays(k, d, back), functools.partial(chain, k, d, back), False)
+                for j in later(k):
+                    own_send(j, d, (room[d] == back) & (room[d] > free(j)))
 
     @scoped
     def arrive(k):
@@ -485,7 +504,7 @@
     mix()
     for k in range(up_parts, parts):
         for d in ways:
-            own_send(k, d, room[d] == 0)
+            own_send(k, d, room[d] <= free(k))
     for b in range(1, n):
         gelu(b)
     for c in range(up_parts):
@@ -493,11 +512,10 @@
 
     def bias_send(j):
         to = lax.rem(dp + j, dp_size)
-        return send(kb.at[dp], kb.at[dp], kbs.at[j], kbr.at[dp], (to, me))
-
-    def bias_arrive(j):
-        src = lax.rem(dp + j, dp_size)
-        return send(kb.at[src], kb.at[src], kbs.at[j], kbr.at[src], (src, me))
+        return send(kb.at[dp], kb.at[dp], kbs.at[0], kbr.at[0], (to, me))
+
+    def bias_group():
+        return group(kb.at[pl.ds(0, dp_size - 1)], kbs.at[0], kbr.at[0])
 
     sent = 0
 
@@ -524,34 +542,43 @@
     back_dot()
     kb[dp] = bias[...]
     for j in range(1, dp_size):
-        start(None, functools.partial(bias_send, j))
-    for r in range(sum_parts):
-        part_dot(r)
-        z_first(r)
+        start(None, functools.partial(bias_send, j), False)
+    for r in range(0, sum_parts, 2):
+        count = min(2, sum_parts - r)
+        if r + 2 >= sum_parts:
+            grad(up_parts)
+        part_dot(r, count)
+        for j in range(r, r + count):
+            z_first(j, 0)
+    for t in range(1, n - 1):
+        for r in range(sum_parts):
+            z_first(r, t)
     relay_to(parts)
-    summed = 0
+    items = [(r, t) for t in range(1, n - 1) for r in range(sum_parts)]
+    done = 0
     for k in range(up_parts, parts):
-        grad(k)
-        while summed < sum_parts and summed < (k - up_parts):
-            for t in range(1, n - 1):
-                z_step(summed, t)
-            summed += 1
-    while summed < sum_parts:
-        for t in range(1, n - 1):
-            z_step(summed, t)
-        summed += 1
-    tick()
-    for r in range(sum_parts):
-        z_step(r, n - 1)
-
-    @scoped
-    def total_grad():
-        edges = sorted(set(up_at + sum_at + [width]))
+        if k > up_parts or sum_parts < 3:
+            grad(k)
+        goal = len(items) * (k - up_parts + 1) // max(1, mix_parts - 1)
+        for item in items[done:goal]:
+            z_step(*item)
+        done = max(done, min(goal, len(items)))
+
+    def g_edge(r, d):
+        to = (dp, jnp.clip(me + step_of[d], 0, n - 1))
+        lane = pl.ds(sum_at[r], sum_wide[r])
+        src = gpad.at[pl.ds(tokens if d == 0 else EDGE, EDGE), lane]
+        dst = gpad.at[pl.ds(0 if d == 0 else EDGE + tokens, EDGE), lane]
+        return send(src, dst, gs.at[r, d], gr.at[r, d], to)
+
+    @scoped
+    def total_grad(r):
+        edges = sorted({e for e in up_at + [width] if sum_at[r] < e < sum_at[r] + sum_wide[r]})
+        edges = [sum_at[r]] + edges + [sum_at[r] + sum_wide[r]]
         for low, top in zip(edges, edges[1:]):
             c = max(i for i in range(up_parts) if up_at[i] <= low)
-            r = max(i for i in range(sum_parts) if sum_at[i] <= low)
-
-            def sum_step(i, _, low=low, c=c, r=r):
+
+            def sum_step(i, _, low=low, c=c):
                 at = pl.ds(pl.multiple_of(low + i * 128, 128), 128)
                 lane = pl.ds(pl.multiple_of(low - sum_at[r] + i * 128, 128), 128)
                 up_lane = pl.ds(pl.multiple_of(low - up_at[c] + i * 128, 128), 128)
@@ -559,68 +586,42 @@
                 mine = sums[r][block_rows(me), lane].astype(F32)
                 left = jnp.where(me > 0, zrecvs[r][me, :, lane].astype(F32), 0.0)
                 right = jnp.where(me < n - 1, zrecvs[r][n, :, lane].astype(F32), 0.0)
-                gpad[pl.ds(EDGE, tokens), at] = (up + (mine + left + right)).astype(BF16)
+                g = (up + (mine + left + right)).astype(BF16)
+                gpad[pl.ds(EDGE, tokens), at] = g
                 return 0
 
             lax.fori_loop(0, (top - low) // 128, sum_step, 0)
-
-    total_grad()
-
-    def g_edge(d):
-        to = (dp, jnp.clip(me + step_of[d], 0, n - 1))
-        src = gpad.at[pl.ds(tokens if d == 0 else EDGE, EDGE)]
-        dst = gpad.at[pl.ds(0 if d == 0 else EDGE + tokens, EDGE)]
-        return send(src, dst, gs.at[d], gr.at[d], to)
-
-    for d in ways:
-        start(ahead[d] > 0, functools.partial(g_edge, d))
-
-    @scoped
-    def taps():
+        for d in ways:
+            start(ahead[d] > 0, functools.partial(g_edge, r, d))
+
+    @scoped
+    def taps(r):
         def taps_step(i, _):
-            at = pl.ds(pl.multiple_of(i * 128, 128), 128)
+            at = pl.ds(pl.multiple_of(sum_at[r] + i * 128, 128), 128)
             g = gpad[pl.ds(EDGE, tokens), at].astype(F32)
             x = xpad[:, at].astype(F32)
-            sums = [
+            totals = [
                 jnp.sum(g * x[EDGE - 3 + tap : EDGE - 3 + tap + tokens], axis=0, keepdims=True)
                 for tap in range(KW)
             ]
-            sums.append(jnp.zeros_like(sums[0]))
-            kp[i // (width // 256), :, pl.ds(pl.multiple_of(lax.rem(i, width // 256) * 128, 128), 128)] = jnp.concatenate(sums, axis=0)
+            totals.append(jnp.zeros_like(totals[0]))
+            j = i + sum_at[r] // 128
+            lane = pl.ds(pl.multiple_of(lax.rem(j, width // 256) * 128, 128), 128)
+            kp[j // (width // 256), :, lane] = jnp.concatenate(totals, axis=0)
             return 0
 
-        lax.fori_loop(0, width // 128, taps_step, 0)
-
-    taps()
-
-    def pair_taps():
-        return send(kp.at[1 - core], kp.at[2], kps.at[0], kpr.at[0], (partner, me))
-
-    start(None, pair_taps)
-    tick()
-
-    def k1_send(j):
-        to = lax.rem(me + j, n)
-        return send(k1.at[me], k1.at[me], k1s.at[j], k1r.at[me], (dp, to))
-
-    def k1_arrive(j):
-        src = lax.rem(me + j, n)
-        return send(k1.at[src], k1.at[src], k1s.at[j], k1r.at[src], (dp, src))
-
-    pair_taps().wait_recv()
-    k1[me] = kp[core] + kp[2]
-    for j in range(1, n):
-        start(None, functools.partial(k1_send, j))
-    for d in ways:
-
-        @pl.when(room[d] > 0)
-        def _(d=d):
-            g_edge(d).wait_recv()
-
-    @scoped
-    def gin():
+        lax.fori_loop(0, sum_wide[r] // 128, taps_step, 0)
+
+    @scoped
+    def gin(r):
+        for d in ways:
+
+            @pl.when(room[d] > 0)
+            def _(d=d):
+                g_edge(r, d).wait_recv()
+
         def gin_step(i, _):
-            at = pl.ds(pl.multiple_of(i * 128, 128), 128)
+            at = pl.ds(pl.multiple_of(sum_at[r] + i * 128, 128), 128)
             g = gpad[:, at].astype(F32)
             taps = k_ref[:, at]
             total = g[EDGE : EDGE + tokens]
@@ -630,15 +631,39 @@
             gin_ref[:, at] = total.astype(BF16)
             return 0
 
-        lax.fori_loop(0, width // 128, gin_step, 0)
-
-    gin()
+        lax.fori_loop(0, sum_wide[r] // 128, gin_step, 0)
+
+    for r in range(sum_parts):
+        z_step(r, n - 1)
+        total_grad(r)
+        taps(r)
+        if r % 2:
+            tick()
+
+    def pair_taps():
+        return send(kp.at[1 - core], kp.at[2], kps.at[0], kpr.at[0], (partner, me))
+
+    start(None, pair_taps)
+    for r in range(sum_parts - 1):
+        gin(r)
+
+    def k1_send(j):
+        to = lax.rem(me + j, n)
+        return send(k1.at[me], k1.at[me], k1s.at[0], k1r.at[0], (dp, to))
+
+    def k1_group():
+        return group(k1.at[pl.ds(0, n - 1)], k1s.at[0], k1r.at[0])
+
+    pair_taps().wait_recv()
+    k1[me] = kp[core] + kp[2]
+    for j in range(1, n):
+        start(None, functools.partial(k1_send, j), False)
     tick()
+    gin(sum_parts - 1)
 
     @scoped
     def k1_wait():
-        for j in range(1, n):
-            k1_arrive(j).wait_recv()
+        k1_group().wait_recv()
 
     k1_wait()
     taps_sum = k1[0]
@@ -648,20 +673,18 @@
 
     def k2_send(j):
         to = lax.rem(chip + j, chips) * 2 + core
-        return send(k2.at[chip], k2.at[chip], k2s.at[j], k2r.at[chip], (to, me))
-
-    def k2_arrive(j):
-        src = lax.rem(chip + j, chips)
-        return send(k2.at[src], k2.at[src], k2s.at[j], k2r.at[src], (src * 2 + core, me))
+        return send(k2.at[chip], k2.at[chip], k2s.at[0], k2r.at[0], (to, me))
+
+    def k2_group():
+        return group(k2.at[pl.ds(0, chips - 1)], k2s.at[0], k2r.at[0])
 
     for j in range(1, chips):
-        start(None, functools.partial(k2_send, j))
+        start(None, functools.partial(k2_send, j), False)
     tick()
 
     @scoped
     def k2_wait():
-        for j in range(1, chips):
-            k2_arrive(j).wait_recv()
+        k2_group().wait_recv()
 
     k2_wait()
     total = k2[0]
@@ -675,8 +698,7 @@
     start(None, functools.partial(k3_copy, core))
     while active:
         tick()
-    for j in range(1, dp_size):
-        bias_arrive(j).wait_recv()
+    bias_group().wait_recv()
     total = kb[0]
     for j in range(1, dp_size):
         total = total + kb[j]
@@ -689,6 +711,26 @@
 
     @scoped
     def drain():
+        for m in range(n):
+
+            @pl.when(me == m)
+            def _(m=m):
+                for k in range(parts):
+                    for d in ways:
+                        count = sent_of(m, k, d)
+                        if count:
+                            ref = gathers[k].at[pl.ds(0, count * tokens)]
+                            group(ref, us.at[k, d], ur.at[k, 0]).wait_send()
+
+        for w in range(parts):
+            group(finals[w].at[:, :, pl.ds(0, chips - 1)], rs.at[w], rr.at[w, 0]).wait_send()
+            group(finals[w].at[1 - core], ds.at[w], dr.at[w]).wait_send()
+        for r in range(sum_parts):
+            ref = sums[r].at[pl.ds(0, (n - 1) * tokens)]
+            group(ref, zs.at[r], zr.at[r, 0]).wait_send()
+        bias_group().wait_send()
+        k1_group().wait_send()
+        k2_group().wait_send()
         for cond, make in pending:
             if cond is None:
                 make().wait_send()
@@ -750,16 +792,16 @@
             pltpu.VMEM((2, 8, width // 2), F32),
             dma((3,)), dma((n,)), dma((up_parts,)),
             dma((2,)), dma((2,)),
-            dma((parts, 2, n)), dma((parts, 2)), dma((parts, 2, n)),
-            dma((sum_parts, 2, n)), dma((sum_parts, 2, n)),
+            dma((parts, 2)), dma((parts, n)),
+            dma((sum_parts,)), dma((sum_parts, n + 1)),
             dma((parts,)), dma((parts,)),
-            dma((parts, 2, 2 * bits)), dma((parts, 2, 2 * bits)),
-            dma((parts, 2, bits + 1)), dma((parts, 2, bits + 1)),
-            dma((2,)), dma((2,)),
-            dma((dp_size,)), dma((dp_size,)),
+            dma((parts,)), dma((parts, 2 * bits)),
+            dma((parts,)), dma((parts,)),
+            dma((sum_parts, 2)), dma((sum_parts, 2)),
             dma((1,)), dma((1,)),
-            dma((n,)), dma((n,)),
-            dma((chips,)), dma((chips,)),
+            dma((1,)), dma((1,)),
+            dma((1,)), dma((1,)),
+            dma((1,)), dma((1,)),
             dma((1,)), dma((1,)),
         ],
         compiler_params=pltpu.CompilerParams(

time: 121 us -> 107 us (0.88)
  Pallas kernels: 117 us -> 103 us
    pallas_call x1, Pallas kernels: 112 us -> 97.4 us  [shards(): pl.pallas_call(functools.partial(body, n, dp_size, up_wide, mix_wide, sum...]
where the time goes in v2:
time: 107 us
  Pallas kernels  103 us (96%)
  local copies, waits for them, and re-layouts  2.83 us (3%)
    pallas_call x1, Pallas kernels, shards(): pl.pallas_call(functools.partial(body, n, dp_size, up_wide, mix_wide, sum...  97.4 us
    pallas_call x1, Pallas kernels, shards(): pl.pallas_call(functools.partial(widen, up_wide, mix_wide), out_shape=[sh...  5.59 us
    unnamed x6, local copies, waits for them, and re-layouts  2.83 us

profile of v2, /device:TPU:1, one launch (start us, length us, event | category | flops | bytes accessed | tf_op | source)
XLA Modules:
  0.0 106.6 jit_solution(5180089709215008640)
XLA Ops:
  0.6 0.0 copy-start
  0.6 1.0 copy-done
  1.7 0.0 copy-start.1
  1.7 1.0 copy-done.1
  2.7 0.0 copy-start.2
  2.7 0.8 copy-done.2
  3.5 97.4 %shard_map.101 = (bf16[192,1280]{1,0:T(8,128)(2,1)S(1)}, f32[7,1280]{1,0:T(8,128)S(1)}, f32[1,1280]{1,0:T(1,128)S(1)}, bf16[2,2,4,80,256]{4,3,2,1,0:T(8,128)(2,1...) custom-call(bf16[192,1280]{1,0:T(8,128)(2,1)S(1)} %bitcast.23, ...), custom_call_target="tpu_custom_call" | custom-call | tf_op jit(solution)/shard_map/pallas_call | solution.py:767
  100.8 5.6 %shard_map.102 = (bf16[1,192,1280]{2,1,0:T(8,128)(2,1)}, f32[1280,1280]{1,0:T(8,128)}, f32[1280,1280]{1,0:T(8,128)}, f32[1280]{0:T(1024)}, f32[7,1280]{1,0:T(8,128)}) custom-call(bf16[1280,256]{1,0:T(8,128)(2,1)S(1)} %bitcast.13, bf16[1280,256]{1,0:T(8,128)(2,1)S(1)} %bitcast.14, bf16[1280,256]{1,0:T(8,128)(2,1)S(1)} %bitcast.15, ...), custom_call_target="tpu_custom_call" | custom-call | tf_op jit(solution)/shard_map/pallas_call | solution.py:821
Async XLA Ops:
  0.6 1.0 copy-start
  1.7 1.0 copy-start.1
  2.7 0.8 copy-start.2

commit v3 on v2

--- a/solution.py
+++ b/solution.py
@@ -637,13 +637,14 @@
         z_step(r, n - 1)
         total_grad(r)
         taps(r)
-        if r % 2:
+        if r == 1:
             tick()
 
     def pair_taps():
         return send(kp.at[1 - core], kp.at[2], kps.at[0], kpr.at[0], (partner, me))
 
     start(None, pair_taps)
+    tick()
     for r in range(sum_parts - 1):
         gin(r)
 
@@ -853,7 +854,7 @@
 
     def widen_one(source, target):
         high = target.shape[0]
-        step = 64
+        step = 128
 
         def widen_step(i, _):
             at = pl.ds(pl.multiple_of(i * step, step), step)

time: 107 us -> 106 us (level)
  no operation moved by 1% of the time
where the time goes in v3:
time: 106 us
  Pallas kernels  102 us (96%)
  local copies, waits for them, and re-layouts  2.83 us (3%)
    pallas_call x1, Pallas kernels, shards(): pl.pallas_call(functools.partial(body, n, dp_size, up_wide, mix_wide, sum...  96.8 us
    pallas_call x1, Pallas kernels, shards(): pl.pallas_call(functools.partial(widen, up_wide, mix_wide), out_shape=[sh...  5.59 us
    unnamed x6, local copies, waits for them, and re-layouts  2.83 us

profile of v3, /device:TPU:1, one launch (start us, length us, event | category | flops | bytes accessed | tf_op | source)
XLA Modules:
  0.0 106.0 jit_solution(6312770855812254379)
XLA Ops:
  0.6 0.0 copy-start
  0.6 1.0 copy-done
  1.7 0.0 copy-start.1
  1.7 1.0 copy-done.1
  2.7 0.0 copy-start.2
  2.7 0.8 copy-done.2
  3.5 96.8 %shard_map.101 = (bf16[192,1280]{1,0:T(8,128)(2,1)S(1)}, f32[7,1280]{1,0:T(8,128)S(1)}, f32[1,1280]{1,0:T(1,128)S(1)}, bf16[2,2,4,80,256]{4,3,2,1,0:T(8,128)(2,1...) custom-call(bf16[192,1280]{1,0:T(8,128)(2,1)S(1)} %bitcast.23, ...), custom_call_target="tpu_custom_call" | custom-call | tf_op jit(solution)/shard_map/pallas_call | solution.py:768
  100.3 5.6 %shard_map.102 = (bf16[1,192,1280]{2,1,0:T(8,128)(2,1)}, f32[1280,1280]{1,0:T(8,128)}, f32[1280,1280]{1,0:T(8,128)}, f32[1280]{0:T(1024)}, f32[7,1280]{1,0:T(8,128)}) custom-call(bf16[1280,256]{1,0:T(8,128)(2,1)S(1)} %bitcast.13, bf16[1280,256]{1,0:T(8,128)(2,1)S(1)} %bitcast.14, bf16[1280,256]{1,0:T(8,128)(2,1)S(1)} %bitcast.15, ...), custom_call_target="tpu_custom_call" | custom-call | tf_op jit(solution)/shard_map/pallas_call | solution.py:822
Async XLA Ops:
  0.6 1.0 copy-start
  1.7 1.0 copy-start.1
  2.7 0.8 copy-start.2

commit v4 on v3

--- a/solution.py
+++ b/solution.py
@@ -644,7 +644,6 @@
         return send(kp.at[1 - core], kp.at[2], kps.at[0], kpr.at[0], (partner, me))
 
     start(None, pair_taps)
-    tick()
     for r in range(sum_parts - 1):
         gin(r)
 
@@ -659,7 +658,7 @@
     k1[me] = kp[core] + kp[2]
     for j in range(1, n):
         start(None, functools.partial(k1_send, j), False)
-    tick()
+    tick(2)
     gin(sum_parts - 1)
 
     @scoped

time: 106 us -> 106 us (level)
  no operation moved by 1% of the time
where the time goes in v4:
time: 106 us
  Pallas kernels  102 us (96%)
  local copies, waits for them, and re-layouts  2.83 us (3%)
    pallas_call x1, Pallas kernels, shards(): pl.pallas_call(functools.partial(body, n, dp_size, up_wide, mix_wide, sum...  96.7 us
    pallas_call x1, Pallas kernels, shards(): pl.pallas_call(functools.partial(widen, up_wide, mix_wide), out_shape=[sh...  5.59 us
    unnamed x6, local copies, waits for them, and re-layouts  2.83 us

profile of v4, /device:TPU:1, one launch (start us, length us, event | category | flops | bytes accessed | tf_op | source)
XLA Modules:
  0.0 105.9 jit_solution(7265637888496543734)
XLA Ops:
  0.6 0.0 copy-start
  0.6 1.0 copy-done
  1.7 0.0 copy-start.1
  1.7 1.0 copy-done.1
  2.7 0.0 copy-start.2
  2.7 0.8 copy-done.2
  3.5 96.7 %shard_map.101 = (bf16[192,1280]{1,0:T(8,128)(2,1)S(1)}, f32[7,1280]{1,0:T(8,128)S(1)}, f32[1,1280]{1,0:T(1,128)S(1)}, bf16[2,2,4,80,256]{4,3,2,1,0:T(8,128)(2,1...) custom-call(bf16[192,1280]{1,0:T(8,128)(2,1)S(1)} %bitcast.23, ...), custom_call_target="tpu_custom_call" | custom-call | tf_op jit(solution)/shard_map/pallas_call | solution.py:767
  100.2 5.6 %shard_map.102 = (bf16[1,192,1280]{2,1,0:T(8,128)(2,1)}, f32[1280,1280]{1,0:T(8,128)}, f32[1280,1280]{1,0:T(8,128)}, f32[1280]{0:T(1024)}, f32[7,1280]{1,0:T(8,128)}) custom-call(bf16[1280,256]{1,0:T(8,128)(2,1)S(1)} %bitcast.13, bf16[1280,256]{1,0:T(8,128)(2,1)S(1)} %bitcast.14, bf16[1280,256]{1,0:T(8,128)(2,1)S(1)} %bitcast.15, ...), custom_call_target="tpu_custom_call" | custom-call | tf_op jit(solution)/shard_map/pallas_call | solution.py:821
Async XLA Ops:
  0.6 1.0 copy-start
  1.7 1.0 copy-start.1
  2.7 0.8 copy-start.2
